TPU v7x, 512 devices: a whole 4x4x16 slice. The times are simulated.
512 devices in a mesh: row: 16 (over x, z_hi), col: 8 (over y, core), layer: 4 (over z_lo).
Axes of the slice: x: 4, y: 4, z: 16 (z_hi: 4, z_lo: 4; z = z_hi * 4 + z_lo), core: 2. Of those that a mesh axis runs over, the one named last changes fastest.
Arguments:
- design: float32 [4096, 8192], P(('row', 'layer'), 'col'), may hold values from -6 to 6
- responses: float32 [4096, 8192], P(('row', 'layer'), 'col'), may hold values from -0.09375 to 0.09375
Outputs:
- normal_update: float32 [8192, 8192], P('row', ('col', 'layer'))
All inputs are finite; a program needn't handle non-finite values.
Results may differ from a plain program's by a relative error of at most 0.00008.
Values sent between devices are 32-bit elements; how exact they have to be, the bound alone decides.
A program may use at most 64 MiB of HBM per device.

v0:
```python
import jax
import jax.numpy as jnp
from jax import lax
from jax.sharding import Mesh
from jax.sharding import PartitionSpec as P

ROW = ("row_0", "row_1")
ROW_LAYER = ("row_0", "row_1", "layer")


HIGHEST = lax.Precision.HIGHEST


def in_order(blocks, dim):
    blocks = jnp.moveaxis(blocks, 0, dim)
    shape = blocks.shape
    return blocks.reshape(*shape[:dim], shape[dim] * shape[dim + 1], *shape[dim + 2 :])


def copy_for_each(array, axis):
    devices = lax.axis_size(axis)
    return lax.all_to_all(
        jnp.broadcast_to(array[None], (devices, *array.shape)), axis, 0, 0, tiled=True
    )


def gathered_copies(array, axis, dim):
    return in_order(copy_for_each(array, axis), dim)


def gathered_by_axis(array, axes, dim):
    result = array
    for number in range(len(axes) - 1, -1, -1):
        result = lax.all_gather(result, axes[number], axis=dim, tiled=True)
    return result


def in_blocks(array, dim, devices):
    before, after = (array.shape[:dim], array.shape[dim + 1 :])
    return jnp.moveaxis(array.reshape(*before, devices, -1, *after), dim, 0)


def summed_on_arrival(array, axis, dim):
    devices = lax.axis_size(axis)
    blocks = lax.all_to_all(in_blocks(array, dim, devices), axis, 0, 0, tiled=True)
    return jnp.sum(blocks, axis=0)


def body(design, responses):
    widened = gathered_copies(design, "col", 1)
    design_panel = lax.all_to_all(widened, ROW, split_axis=1, concat_axis=0, tiled=True)
    partial_value = lax.dot_general(
        design_panel,
        gathered_by_axis(responses, ROW, 0),
        (((0,), (0,)), ((), ())),
        precision=HIGHEST,
        preferred_element_type=jnp.float32,
    )
    result = summed_on_arrival(partial_value, "layer", 1)
    return result


def solution(mesh):
    finer = Mesh(
        mesh.devices.reshape(4, 4, mesh.shape["col"], mesh.shape["layer"]),
        ("row_0", "row_1", "col", "layer"),
    )
    in_specs = (P(ROW_LAYER, "col"), P(ROW_LAYER, "col"))
    out_specs = P(ROW, ("col", "layer"))
    return jax.shard_map(body, mesh=finer, in_specs=in_specs, out_specs=out_specs, check_vma=False)
```

profile of v0, /device:TPU:1, one launch (start us, length us, event | category | flops | bytes accessed | tf_op | source)
XLA Modules:
  0.0 280.1 jit_solution(7640119688048867498)
XLA Ops:
  6.5 2.6 broadcast_in_dim.2
  9.1 10.3 %all-to-all-start = ((f32[8,64,1024]{2,1,0:T(8,128)}), f32[8,64,1024]{2,1,0:T(8,128)S(1)}, u32[]{:S(2)}, u32[]{:S(2)}) async-start(f32[8,64,1024]{2,1,0:T(8,128)} %broadcast_in_dim.2), calls=%async_computation | async-start | bytes 4194304 | tf_op jit(solution)/shard_map/all_to_all | solution.py:22
  19.4 0.0 all-gather.3.cloned.1.call-start
  19.4 0.7 all-gather.3.cloned.1.call-update
  20.2 25.5 %all-to-all-done = f32[8,64,1024]{2,1,0:T(8,128)S(1)} async-done(((f32[8,64,1024]{2,1,0:T(8,128)}), f32[8,64,1024]{2,1,0:T(8,128)S(1)}, u32[]{:S(2)}, u32[]{:S(2)}) %all-to-all-start) | async-done | bytes 2097184 | tf_op jit(solution)/shard_map/all_to_all | solution.py:22
  45.7 2.6 copy.7
  48.2 1.7 all_to_all.21
  50.0 2.6 copy.8
  52.6 13.1 %all-to-all-start.1 = ((f32[64,16,512]{2,0,1:T(8,128)}), f32[64,16,512]{2,0,1:T(8,128)S(1)}, u32[]{:S(2)}, u32[]{:S(2)}) async-start(f32[64,16,512]{2,0,1:T(8,128)} %copy.8), calls=%async_computation.1 | async-start | bytes 4194304 | tf_op jit(solution)/shard_map/all_to_all | solution.py:51
  65.6 0.0 all-gather.5.cloned.1.call-start
  65.7 34.2 %all-gather.3.cloned.1.call-done = f32[256,1024]{1,0:T(8,128)} async-done(((f32[64,1024]{1,0:T(8,128)}), f32[256,1024]{1,0:T(8,128)}) %all-gather.3.cloned.1.call-update) | async-done | bytes 1048592 | tf_op jit(solution)/shard_map/all_gather | solution.py:34
  99.9 0.0 all-gather.5.cloned.1.call-update
  100.0 98.6 %all-gather.5.cloned.1.call-done = f32[1024,1024]{1,0:T(8,128)} async-done(((f32[256,1024]{1,0:T(8,128)}), f32[1024,1024]{1,0:T(8,128)}) %all-gather.5.cloned.1.call-update) | async-done | bytes 4194320 | tf_op jit(solution)/shard_map/all_gather | solution.py:34
  198.5 5.4 %copy.9 = f32[1024,1024]{1,0:T(8,128)} copy(f32[1024,1024]{0,1:T(8,128)} %bitcast.15) | data formatting | bytes 8388608 | tf_op jit(solution)/shard_map/dot_general | solution.py:52
  203.9 0.0 all-to-all-done.1
  203.9 15.0 %convolution_bitcast_fusion = f32[4,512,256]{2,1,0:T(8,128)S(1)} fusion(f32[1024,512,1]{1,0,2:T(8,128)S(1)} %bitcast.14, f32[4,256,1024]{2,1,0:T(8,128)} %bitcast.12), kind=kOutput, calls=%fused_computation | convolution fusion | flops 6442450944 | bytes 8388608 | tf_op jit(solution)/shard_map/dot_general | solution.py:52
  218.9 53.4 %all_to_all.29 = f32[4,512,256]{2,1,0:T(8,128)S(1)} all-to-all(f32[4,512,256]{2,1,0:T(8,128)S(1)} %convolution_bitcast_fusion), channel_id=1, replica_groups=mesh['row_0'=4,'row_1'=4,'col'=8,'layer'=4] {'layer'}, dimensions={0} | all-to-all | bytes 4194304 | tf_op jit(solution)/shard_map/all_to_all | solution.py:45
  272.3 1.0 reduce_sum.9
Async XLA Ops:
  9.1 36.6 %all-to-all-start = ((f32[8,64,1024]{2,1,0:T(8,128)}), f32[8,64,1024]{2,1,0:T(8,128)S(1)}, u32[]{:S(2)}, u32[]{:S(2)}) async-start(f32[8,64,1024]{2,1,0:T(8,128)} %broadcast_in_dim.2), calls=%async_computation | async-start | bytes 4194304 | tf_op jit(solution)/shard_map/all_to_all | solution.py:22
  19.4 80.5 %all-gather.3.cloned.1.call-start = ((), (), s32[]{:S(2)}) async-start(), calls=%async_computation.3 | async-start | bytes 1310720 | tf_op jit(solution)/shard_map/all_gather | solution.py:34
  52.6 151.4 %all-to-all-start.1 = ((f32[64,16,512]{2,0,1:T(8,128)}), f32[64,16,512]{2,0,1:T(8,128)S(1)}, u32[]{:S(2)}, u32[]{:S(2)}) async-start(f32[64,16,512]{2,0,1:T(8,128)} %copy.8), calls=%async_computation.1 | async-start | bytes 4194304 | tf_op jit(solution)/shard_map/all_to_all | solution.py:51
  65.6 132.9 %all-gather.5.cloned.1.call-start = ((), (), s32[]{:S(2)}) async-start(), calls=%async_computation.4 | async-start | bytes 5242880 | tf_op jit(solution)/shard_map/all_gather | solution.py:34
Sparse Core Ops, SparseCore 0:
  22.3 77.5 all-gather.2
  102.0 96.4 all-gather.4
where the time goes:
time: 281 us; the launch traced here: 280 us
  waiting for transfers between devices  159 us (57%)
  blocking collectives  53.4 us (19%)
  starting transfers between devices  23.5 us (8%)
  matrix products  15 us (5%)
  local copies, waits for them, and re-layouts  14.8 us (5%)
  between operations  13.4 us (5%)
    all_gather x2, waiting for transfers between devices, gathered_by_axis(): result = lax.all_gather(result, axes[number], axis=dim, tiled=True)  133 us
    all_to_all x1, blocking collectives, summed_on_arrival(): lax.all_to_all(in_blocks(array, dim, devices), axis, 0, 0, tiled=True)  53.4 us
    all_to_all x1, waiting for transfers between devices, copy_for_each(): lax.all_to_all(jnp.broadcast_to(array[None], (devices, *array.shape)), ax...  25.5 us
    dot_general x1, matrix products, body(): lax.dot_general(design_panel, gathered_by_axis(responses, ROW, 0), (((0,)...  15 us
    all_to_all x1, starting transfers between devices, body(): lax.all_to_all(widened, ROW, split_axis=1, concat_axis=0, tiled=True)  13.1 us
    all_to_all x1, starting transfers between devices, copy_for_each(): lax.all_to_all(jnp.broadcast_to(array[None], (devices, *array.shape)), ax...  10.3 us
  transfers between devices with their start and end apart: 4, of which 3 were waited for; matrix products, arithmetic and copies ran while one was open for 4% of the time, Pallas kernels for 0%

commit v1 on v0

v1 whole, which is shorter than its diff:
```python
import jax
import jax.numpy as jnp
from jax import lax
from jax.experimental import pallas as pl
from jax.experimental.pallas import tpu as pltpu
from jax.sharding import Mesh
from jax.sharding import PartitionSpec as P

MESH = pl.DeviceIdType.MESH
F32, BF16 = jnp.float32, jnp.bfloat16


def split(value):
    high = value.astype(BF16)
    return high, (value - high.astype(F32)).astype(BF16)


PIECES = (
    [(64 * s, 64) for s in range(8)]
    + [(512, 32)]
    + [(64 * s, 64) for s in range(9, 16)]
    + [(544, 32)]
)
DIRECT = [15, 1, 14, 2, 13, 3, 12, 4]
RELAYED = [11, 5, 10, 6, 9, 7, 16, 8]


def kernel(d_hbm, r_hbm, o_ref, dv, rv, turned, dbuf, rbuf, dth, dtl, local, ss, dz, dy, dd, tz, rz, rx):
    x, zh, y, c, p = (lax.axis_index(n) for n in ("x", "zh", "y", "c", "p"))
    z = 4 * zh + p

    def ring(v, n):
        return lax.rem(v + 4 * n, n)

    def at_z(d):
        w = ring(z + d, 16)
        return {"zh": lax.div(w, 4), "p": lax.rem(w, 4)}

    up_x, down_x = {"x": ring(x + 1, 4)}, {"x": ring(x - 1, 4)}
    up_y, down_y = {"y": ring(y + 1, 4)}, {"y": ring(y - 1, 4)}
    partner = {"c": 1 - c}

    started = []

    def send(src, dst, sem, device, when=None):
        number = len(started)
        copy = pltpu.make_async_remote_copy(
            src_ref=src,
            dst_ref=dst,
            send_sem=ss.at[number],
            recv_sem=sem,
            device_id=device,
            device_id_type=MESH,
        )
        started.append((copy, when))
        if when is None:
            copy.start()
        else:
            pl.when(when)(copy.start)

    def arrived(dst, sem, when=None):
        copy = pltpu.make_async_copy(dst, dst, sem)
        if when is None:
            copy.wait()
        else:
            pl.when(when)(copy.wait)

    load_d = pltpu.make_async_copy(d_hbm, dv, local.at[0])
    load_r = pltpu.make_async_copy(r_hbm, rv, local.at[1])
    own = r_hbm.at[:, pl.ds(pl.multiple_of(p * 256, 256), 256)]
    load_own = pltpu.make_async_copy(own, rbuf.at[x, pl.ds(0, 64)], local.at[2])
    load_d.start()
    load_r.start()
    load_own.start()

    barrier = pltpu.get_barrier_semaphore()

    def greet(device, when=None):
        def signal():
            pl.semaphore_signal(barrier, inc=1, device_id=device, device_id_type=MESH)

        if when is None:
            signal()
        else:
            pl.when(when)(signal)

    source_core = lax.div(zh, 2)
    for d in (1, -1, 2, -2, 3, -3, 4, -4):
        greet(at_z(d))
    for device in (up_x, down_x, up_y, down_y, partner):
        greet(device)
    for other in range(4):
        greet({"x": other, "y": x}, jnp.logical_or(x != other, y != x))

    def origin(r, ps):
        return {"zh": ring(zh - r, 4), "p": ps, "c": source_core}

    def upward(r, ps):
        return r == 1 or (r == 2 and ps >= 2)

    for r in (1, 3, 2):
        for ps in range(4):
            greet(origin(r, ps), p == (0 if upward(r, ps) else 3))
    diagonal = x == y
    holder = c == source_core
    pl.semaphore_wait(
        barrier,
        4 - diagonal.astype(jnp.int32) + 8 + 5 + jnp.where(holder, 2, 4),
    )

    load_d.wait()
    for part in range(4):
        send(
            dv.at[pl.ds(16 * part, 16)],
            turned.at[x],
            tz.at[x],
            {"x": y, "y": part},
            jnp.logical_or(x != y, y != part),
        )

    @pl.when(diagonal)
    def _():
        turned[x] = dv[pl.ds(pl.multiple_of(16 * y, 16), 16), :]

    def piece(number, owner, rows=None):
        first, count = PIECES[number]
        if rows is not None:
            first, count = first + rows * (count // 2), count // 2
        return rbuf.at[owner, pl.ds(first, count)]

    def along_x(number):
        for side, device in ((0, up_x), (1, down_x)):
            send(piece(number, x), piece(number, x), rx.at[side, number], device)

    load_own.wait()
    along_x(0)
    load_r.wait()
    for d in (1, -1, 2, -2, 3, -3, 4, -4):
        quarter = pl.ds(pl.multiple_of(ring(p + d, 4) * 256, 256), 256)
        slot = (-d) % 16
        send(rv.at[:, quarter], piece(slot, x), rz.at[slot], at_z(d))

    for other in range(4):
        arrived(
            turned.at[other],
            tz.at[other],
            jnp.logical_or(x != other, y != x),
        )

    def block(core, slot):
        return dbuf.at[core, pl.ds(4 * slot, 4), y]

    for h in range(2):
        target = 2 * c + h
        rel = ring(target - zh, 4)
        up = jnp.logical_or(rel == 1, jnp.logical_and(rel == 2, p >= 2))
        entry = jnp.where(rel == 0, p, jnp.where(up, 0, 3))
        slot = 4 * rel + p
        for core in range(2):
            columns = pl.ds(512 * h + 256 * core, 256)
            mine = jnp.logical_and(rel == 0, c == core)
            send(
                turned.at[:, :, columns],
                block(core, slot),
                dz.at[slot],
                {"zh": target, "p": entry, "c": core},
                jnp.logical_not(mine),
            )

            @pl.when(mine)
            def _():
                dbuf[core, pl.ds(4 * p, 4), y] = turned[:, :, columns]

    above, below = at_z(1), at_z(-1)

    def design_slot(r, ps):
        slot = 4 * r + ps
        here = block(c, slot)
        if r == 0:
            arrived(here, dz.at[slot], jnp.logical_not(jnp.logical_and(p == ps, holder)))
            goes_up = jnp.logical_and(p >= ps, p < 3) if ps < 3 else None
            goes_down = jnp.logical_and(p <= ps, p > 0) if ps > 0 else None
        else:
            arrived(here, dz.at[slot])
            goes_up = p < 3 if upward(r, ps) else None
            goes_down = None if upward(r, ps) else p > 0
        if goes_up is not None:
            send(here, here, dz.at[slot], above, goes_up)
        if goes_down is not None:
            send(here, here, dz.at[slot], below, goes_down)

    def group(core, r, part, half=None):
        first, count = (16 * r, 16) if half is None else (16 * r + 8 * half, 8)
        return dbuf.at[core, pl.ds(first, count), part]

    y_of = [y, ring(y - 1, 4), ring(y + 1, 4), ring(y + 2, 4)]

    def to_partner(r, which):
        send(group(c, r, y_of[which]), group(c, r, y_of[which]), dd.at[r, which], partner)

    def along_y(r):
        send(group(c, r, y), group(c, r, y), dy.at[0, r], up_y)
        send(group(c, r, y), group(c, r, y), dy.at[1, r], down_y)
        to_partner(r, 0)

    def relay_y(r):
        arrived(group(c, r, y_of[1]), dy.at[0, r])
        send(group(c, r, y_of[1], 0), group(c, r, y_of[1], 0), dy.at[2, r], up_y)
        to_partner(r, 1)
        arrived(group(c, r, y_of[2]), dy.at[1, r])
        send(group(c, r, y_of[2], 1), group(c, r, y_of[2], 1), dy.at[3, r], down_y)
        to_partner(r, 2)

    def last_y(r):
        arrived(group(c, r, y_of[3], 0), dy.at[2, r])
        arrived(group(c, r, y_of[3], 1), dy.at[3, r])
        to_partner(r, 3)

    left, right, far = ring(x - 1, 4), ring(x + 1, 4), ring(x + 2, 4)

    def from_z(number):
        arrived(piece(number, x), rz.at[number])
        along_x(number)

    def relay_z(number):
        if number >= 12:
            there = 16 if number == 12 else number - 4
            half = 1 if number == 12 else None
            device = at_z(4)
        else:
            there = number + 4
            half = 0 if number == 4 else None
            device = at_z(-4)
        send(piece(number, x, half), piece(there, x), rz.at[there], device)

    def relay_x(number):
        arrived(piece(number, left), rx.at[0, number])
        send(piece(number, left, 0), piece(number, left, 0), rx.at[2, number], up_x)
        arrived(piece(number, right), rx.at[1, number])
        send(piece(number, right, 1), piece(number, right, 1), rx.at[3, number], down_x)

    def last_x(number):
        arrived(piece(number, far, 0), rx.at[2, number])
        arrived(piece(number, far, 1), rx.at[3, number])

    def prepare(r):
        for which in range(4):
            arrived(group(1 - c, r, y_of[which]), dd.at[r, which])

        @pl.loop(0, 4)
        def _(ps):
            slot = 4 * r + ps
            for half in range(2):
                value = dbuf[half, pl.ds(4 * slot, 4)].reshape(256, 256).T
                high, low = split(value)
                dth[slot, pl.ds(256 * half, 256), :] = high
                dtl[slot, pl.ds(256 * half, 256), :] = low

    def multiply(slot):
        owner = ring(z + slot, 16)
        other = 4 * ring(zh - lax.div(owner, 4), 4) + lax.rem(owner, 4)
        rows = pl.ds(pl.multiple_of(64 * slot, 64), 64)
        high, low = split(rbuf[:, rows, :].reshape(256, 256))
        dh, dl = dth[other], dtl[other]
        o_ref[...] += (
            jnp.dot(dh, high, preferred_element_type=F32)
            + jnp.dot(dl, high, preferred_element_type=F32)
            + jnp.dot(dh, low, preferred_element_type=F32)
        )

    o_ref[...] = jnp.zeros_like(o_ref)
    for number in (15, 1):
        from_z(number)
    for ps in range(4):
        design_slot(0, ps)
    along_y(0)
    for number in (14, 2):
        from_z(number)
    for ps in (3, 2, 1, 0):
        design_slot(1, ps)
        design_slot(3, 3 - ps)
    along_y(1)
    along_y(3)
    for number in (13, 3, 12, 4):
        from_z(number)
    for ps in (1, 2, 0, 3):
        design_slot(2, ps)
    along_y(2)
    for number in DIRECT:
        relay_z(number)
    relay_y(0)
    for number in (0, 15, 1, 14, 2):
        relay_x(number)
    relay_y(1)
    relay_y(3)
    for number in (13, 3, 12, 4):
        relay_x(number)
    last_y(0)
    for number in RELAYED[:2]:
        from_z(number)
    last_y(1)
    relay_y(2)
    last_y(3)
    prepare(0)
    for number in RELAYED[2:4]:
        from_z(number)
    for number in RELAYED[:2]:
        relay_x(number)
    last_y(2)
    prepare(1)
    prepare(3)
    for number in RELAYED[4:6]:
        from_z(number)
    for number in RELAYED[2:4]:
        relay_x(number)
    for number in [0, *DIRECT]:
        last_x(number)
    prepare(2)

    @pl.loop(0, 5)
    def _(slot):
        multiply(slot)

    for number in RELAYED[6:8]:
        from_z(number)
    for number in RELAYED[4:6]:
        relay_x(number)

    @pl.loop(12, 16)
    def _(slot):
        multiply(slot)

    for number in RELAYED[:4]:
        last_x(number)
    for number in RELAYED[6:8]:
        relay_x(number)
    for first in (5, 10):

        @pl.loop(first, first + 2)
        def _(slot):
            multiply(slot)

    for number in RELAYED[4:]:
        last_x(number)

    @pl.loop(7, 10)
    def _(slot):
        multiply(slot)

    for copy, when in started:
        if when is None:
            copy.wait_send()
        else:
            pl.when(when)(copy.wait_send)


def body(design, responses):
    dma = pltpu.SemaphoreType.DMA
    return pl.pallas_call(
        kernel,
        out_shape=jax.ShapeDtypeStruct((512, 256), F32),
        in_specs=[pl.BlockSpec(memory_space=pl.ANY)] * 2,
        out_specs=pl.BlockSpec(memory_space=pltpu.VMEM),
        scratch_shapes=[
            pltpu.VMEM((64, 1024), F32),
            pltpu.VMEM((64, 1024), F32),
            pltpu.VMEM((4, 16, 1024), F32),
            pltpu.VMEM((2, 64, 4, 16, 256), F32),
            pltpu.VMEM((4, 1024, 256), F32),
            pltpu.VMEM((16, 512, 256), BF16),
            pltpu.VMEM((16, 512, 256), BF16),
            dma((3,)),
            dma((142,)),
            dma((16,)),
            dma((4, 4)),
            dma((4, 4)),
            dma((4,)),
            dma((17,)),
            dma((4, 17)),
        ],
        compiler_params=pltpu.CompilerParams(
            collective_id=0, has_side_effects=True, vmem_limit_bytes=60 * 2**20
        ),
    )(design, responses)


def solution(mesh):
    finer = Mesh(
        mesh.devices.reshape(4, 4, 4, 2, 4), ("x", "zh", "y", "c", "p")
    )
    spec = P(("x", "zh", "p"), ("y", "c"))
    return jax.shard_map(
        body,
        mesh=finer,
        in_specs=(spec, spec),
        out_specs=P(("x", "zh"), ("y", "c", "p")),
        check_vma=False,
    )
```

time: 281 us -> 207 us (0.74)
  the two profiles are of different devices: /device:TPU:1 before, /device:TPU:352 now
where the time goes in v1:
time: 207 us
  Pallas kernels  205 us (99%)
    pallas_call x1, Pallas kernels, body(): pl.pallas_call(kernel, out_shape=jax.ShapeDtypeStruct((512, 256), F32), i...  205 us

profile of v1, /device:TPU:352, one launch (start us, length us, event | category | flops | bytes accessed | tf_op | source)
XLA Modules:
  0.0 207.3 jit_solution(1440051860005314752)
XLA Ops:
  0.0 205.4 %shard_map.28 = f32[512,256]{1,0:T(8,128)} custom-call(f32[64,1024]{1,0:T(8,128)} %d_hbm.1, f32[64,1024]{1,0:T(8,128)} %r_hbm.1), custom_call_target="tpu_custom_call" | custom-call | tf_op jit(solution)/shard_map/pallas_call | solution.py:359
  205.4 1.9 copy.4

commit v2 on v0

v2 whole, which is shorter than its diff:
```python
import jax
import jax.numpy as jnp
from jax import lax
from jax.experimental import pallas as pl
from jax.experimental.pallas import tpu as pltpu
from jax.sharding import Mesh
from jax.sharding import PartitionSpec as P

MESH = pl.DeviceIdType.MESH
F32, BF16 = jnp.float32, jnp.bfloat16

X_OWN, Z_SEND, TURNED, D_SEND, D_SLOT, Y_UP, Y_DOWN, Y_LAST = range(8)
R_SLOT, Z_RELAY, X_UP, X_DOWN, X_LAST, PREPARE, MULTIPLY = range(8, 15)
OWN, NEAR, AWAY, FAR = range(4)

EDGE = [
    (Z_SEND, -1), (Z_SEND, 4), (Z_SEND, 3), (Z_SEND, 1), (Z_SEND, -2), (Z_SEND, -4), (Z_SEND, -3), (Z_SEND, 2), (TURNED,),
    (D_SEND,), (D_SLOT, OWN, 0), (R_SLOT, 14), (D_SLOT, NEAR, 1), (R_SLOT, 15), (X_UP, 14), (D_SLOT, NEAR, 0),
    (D_SLOT, NEAR, 2), (R_SLOT, 12), (R_SLOT, 3), (Z_RELAY, 15), (R_SLOT, 2), (R_SLOT, 4), (Z_RELAY, 2), (D_SLOT, NEAR, 3),
    (D_SLOT, FAR, 3), (X_DOWN, 12), (Z_RELAY, 14), (D_SLOT, OWN, 3), (X_DOWN, 4), (X_DOWN, 3), (Y_DOWN, NEAR, 3),
    (R_SLOT, 1), (Y_UP, OWN, 0), (Y_UP, FAR, 3), (Y_UP, NEAR, 3), (D_SLOT, OWN, 2), (Y_DOWN, NEAR, 0), (R_SLOT, 11),
    (Z_RELAY, 4), (X_DOWN, 14), (X_DOWN, 15), (D_SLOT, OWN, 1), (Y_DOWN, NEAR, 1), (Y_DOWN, OWN, 3), (Y_LAST, NEAR, 3),
    (Y_DOWN, OWN, 2), (X_OWN,), (Y_UP, NEAR, 1), (R_SLOT, 13), (X_LAST, 14), (Y_UP, OWN, 2), (D_SLOT, AWAY, 2),
    (R_SLOT, 6), (X_UP, 12), (X_DOWN, 13), (D_SLOT, AWAY, 3), (D_SLOT, FAR, 2), (X_UP, 4), (X_UP, 2), (R_SLOT, 10),
    (Y_LAST, NEAR, 1), (Y_UP, NEAR, 0), (X_UP, 1), (Y_UP, NEAR, 2), (Z_RELAY, 12), (X_UP, 11), (Z_RELAY, 1), (X_UP, 15),
    (Y_UP, OWN, 3), (R_SLOT, 8), (Y_DOWN, OWN, 1), (X_UP, 0), (Y_DOWN, NEAR, 2), (Y_UP, OWN, 1), (X_UP, 13),
    (Y_LAST, OWN, 1), (Y_UP, AWAY, 2), (X_DOWN, 1), (R_SLOT, 16), (X_DOWN, 6), (X_UP, 6), (Y_DOWN, AWAY, 2),
    (Y_DOWN, OWN, 0), (X_DOWN, 11), (D_SLOT, AWAY, 1), (Y_DOWN, AWAY, 3), (D_SLOT, AWAY, 0), (X_LAST, 12), (Z_RELAY, 13),
    (Y_LAST, NEAR, 0), (X_DOWN, 0), (Y_LAST, NEAR, 2), (R_SLOT, 5), (PREPARE, NEAR), (X_LAST, 1), (Y_DOWN, FAR, 2),
    (X_UP, 10), (X_DOWN, 2), (Z_RELAY, 3), (D_SLOT, FAR, 0), (Y_DOWN, AWAY, 0), (Y_LAST, OWN, 2), (X_LAST, 15),
    (X_DOWN, 10), (X_UP, 3), (Y_UP, AWAY, 3), (X_LAST, 13), (Y_UP, FAR, 2), (R_SLOT, 9), (Y_UP, AWAY, 1), (Y_DOWN, FAR, 3),
    (X_UP, 5), (Y_DOWN, AWAY, 1), (X_DOWN, 5), (X_LAST, 0), (Y_UP, AWAY, 0), (X_LAST, 2), (X_LAST, 4), (Y_LAST, AWAY, 2),
    (X_UP, 16), (X_DOWN, 16), (X_LAST, 3), (Y_LAST, OWN, 3), (D_SLOT, FAR, 1), (X_UP, 8), (Y_LAST, AWAY, 3), (X_DOWN, 8),
    (Y_LAST, OWN, 0), (Y_DOWN, FAR, 0), (MULTIPLY, NEAR, 2), (X_LAST, 10), (Y_UP, FAR, 0), (R_SLOT, 7), (PREPARE, OWN),
    (X_UP, 9), (Y_UP, FAR, 1), (Y_DOWN, FAR, 1), (Y_LAST, FAR, 3), (X_DOWN, 9), (MULTIPLY, OWN, 2), (MULTIPLY, OWN, 0),
    (Y_LAST, AWAY, 1), (Y_LAST, FAR, 2), (MULTIPLY, OWN, 3), (Y_LAST, FAR, 0), (Y_LAST, AWAY, 0), (X_LAST, 16),
    (X_LAST, 11), (X_LAST, 6), (X_LAST, 5), (MULTIPLY, NEAR, 0), (MULTIPLY, NEAR, 3), (X_UP, 7), (X_DOWN, 7),
    (MULTIPLY, NEAR, 1), (MULTIPLY, OWN, 1), (Y_LAST, FAR, 1), (X_LAST, 8), (PREPARE, AWAY), (MULTIPLY, AWAY, 0),
    (PREPARE, FAR), (X_LAST, 7), (X_LAST, 9), (MULTIPLY, AWAY, 3), (MULTIPLY, AWAY, 1), (MULTIPLY, FAR, 1),
    (MULTIPLY, FAR, 2), (MULTIPLY, FAR, 3), (MULTIPLY, FAR, 0), (MULTIPLY, AWAY, 2),
]
INNER = [
    (Z_SEND, -1), (Z_SEND, 4), (Z_SEND, -2), (Z_SEND, 3), (Z_SEND, -4), (Z_SEND, 2), (Z_SEND, 1), (Z_SEND, -3), (TURNED,),
    (D_SEND,), (X_OWN,), (D_SLOT, OWN, 1), (D_SLOT, OWN, 0), (D_SLOT, OWN, 2), (R_SLOT, 4), (R_SLOT, 14),
    (D_SLOT, NEAR, 1), (D_SLOT, NEAR, 0), (R_SLOT, 15), (D_SLOT, OWN, 3), (D_SLOT, NEAR, 2), (R_SLOT, 1), (Y_DOWN, OWN, 2),
    (X_DOWN, 0), (D_SLOT, AWAY, 2), (R_SLOT, 2), (D_SLOT, AWAY, 3), (Y_DOWN, OWN, 0), (X_UP, 14), (D_SLOT, NEAR, 3),
    (Z_RELAY, 1), (Y_UP, OWN, 1), (R_SLOT, 13), (Y_UP, OWN, 0), (Y_DOWN, NEAR, 2), (X_DOWN, 2), (Z_RELAY, 2),
    (Y_UP, NEAR, 0), (X_UP, 15), (R_SLOT, 12), (Z_RELAY, 14), (X_DOWN, 15), (R_SLOT, 3), (Y_LAST, OWN, 0), (Y_UP, NEAR, 2),
    (D_SLOT, AWAY, 1), (X_DOWN, 1), (X_UP, 0), (Y_DOWN, NEAR, 0), (Z_RELAY, 15), (X_UP, 3), (Y_UP, OWN, 2), (R_SLOT, 10),
    (D_SLOT, AWAY, 0), (D_SLOT, FAR, 3), (Z_RELAY, 12), (X_DOWN, 12), (Y_DOWN, NEAR, 3), (R_SLOT, 5), (Z_RELAY, 3),
    (Y_DOWN, AWAY, 0), (X_DOWN, 14), (Y_DOWN, AWAY, 2), (Y_UP, NEAR, 3), (Y_UP, AWAY, 0), (X_UP, 1), (X_DOWN, 3),
    (Y_DOWN, OWN, 3), (Y_UP, AWAY, 2), (X_UP, 4), (Y_LAST, NEAR, 0), (X_DOWN, 10), (X_UP, 13), (Y_DOWN, NEAR, 1),
    (X_LAST, 0), (X_DOWN, 4), (Z_RELAY, 4), (X_UP, 5), (D_SLOT, FAR, 0), (R_SLOT, 6), (X_DOWN, 13), (D_SLOT, FAR, 2),
    (X_UP, 12), (Y_UP, AWAY, 1), (R_SLOT, 11), (Y_UP, NEAR, 1), (Y_LAST, AWAY, 2), (X_UP, 6), (Y_DOWN, OWN, 1),
    (Y_UP, AWAY, 3), (Y_LAST, NEAR, 2), (X_LAST, 14), (Y_DOWN, FAR, 0), (R_SLOT, 7), (X_LAST, 1), (Z_RELAY, 13),
    (Y_LAST, OWN, 2), (X_DOWN, 5), (X_LAST, 12), (Y_LAST, NEAR, 3), (D_SLOT, FAR, 1), (R_SLOT, 8), (X_UP, 2),
    (Y_DOWN, AWAY, 3), (X_UP, 10), (R_SLOT, 16), (Y_LAST, NEAR, 1), (Y_UP, OWN, 3), (Y_LAST, OWN, 1), (X_DOWN, 11),
    (X_UP, 7), (X_DOWN, 7), (X_LAST, 3), (Y_DOWN, AWAY, 1), (X_LAST, 4), (Y_LAST, AWAY, 0), (X_LAST, 13), (PREPARE, NEAR),
    (X_LAST, 2), (X_UP, 11), (X_UP, 16), (Y_UP, FAR, 1), (Y_LAST, AWAY, 3), (Y_LAST, OWN, 3), (Y_UP, FAR, 0), (X_DOWN, 6),
    (MULTIPLY, NEAR, 2), (R_SLOT, 9), (X_LAST, 7), (Y_DOWN, FAR, 3), (X_LAST, 15), (X_DOWN, 16), (MULTIPLY, NEAR, 1),
    (X_LAST, 5), (PREPARE, OWN), (Y_DOWN, FAR, 1), (X_UP, 8), (Y_LAST, AWAY, 1), (Y_UP, FAR, 3), (Y_DOWN, FAR, 2),
    (MULTIPLY, OWN, 0), (X_DOWN, 8), (Y_LAST, FAR, 0), (Y_UP, FAR, 2), (X_DOWN, 9), (X_UP, 9), (MULTIPLY, OWN, 3),
    (MULTIPLY, OWN, 1), (X_LAST, 10), (MULTIPLY, NEAR, 3), (X_LAST, 11), (MULTIPLY, OWN, 2), (PREPARE, AWAY),
    (Y_LAST, FAR, 3), (MULTIPLY, AWAY, 0), (X_LAST, 16), (MULTIPLY, AWAY, 1), (X_LAST, 6), (X_LAST, 8), (Y_LAST, FAR, 1),
    (X_LAST, 9), (Y_LAST, FAR, 2), (MULTIPLY, AWAY, 3), (MULTIPLY, AWAY, 2), (MULTIPLY, NEAR, 0), (PREPARE, FAR),
    (MULTIPLY, FAR, 3), (MULTIPLY, FAR, 0), (MULTIPLY, FAR, 2), (MULTIPLY, FAR, 1),
]

PIECES = (
    [(64 * s, 64) for s in range(8)]
    + [(512, 32)]
    + [(64 * s, 64) for s in range(9, 16)]
    + [(544, 32)]
)


def split(value):
    high = value.astype(BF16)
    return high, (value - high.astype(F32)).astype(BF16)


def kernel(d_hbm, r_hbm, o_ref, dv, rv, turned, dbuf, rbuf, dth, dtl, local, ss, tz, dz, dy, dd, rz, rx):
    x, zh, y, c, p = (lax.axis_index(n) for n in ("x", "zh", "y", "c", "p"))
    z = 4 * zh + p

    def ring(v, n):
        return lax.rem(v + 4 * n, n)

    def at_z(d):
        w = ring(z + d, 16)
        return {"zh": lax.div(w, 4), "p": lax.rem(w, 4)}

    up_x, down_x = {"x": ring(x + 1, 4)}, {"x": ring(x - 1, 4)}
    up_y, down_y = {"y": ring(y + 1, 4)}, {"y": ring(y - 1, 4)}
    partner = {"c": 1 - c}
    source_core = lax.div(zh, 2)
    diagonal = x == y
    holder = c == source_core
    low = p < 2

    load_d = pltpu.make_async_copy(d_hbm, dv, local.at[0])
    load_r = pltpu.make_async_copy(r_hbm, rv, local.at[1])
    own = r_hbm.at[:, pl.ds(pl.multiple_of(p * 256, 256), 256)]
    load_own = pltpu.make_async_copy(own, rbuf.at[x, pl.ds(0, 64)], local.at[2])
    load_d.start()
    load_r.start()
    load_own.start()

    barrier = pltpu.get_barrier_semaphore()

    def greet(device, when=None):
        def signal():
            pl.semaphore_signal(barrier, inc=1, device_id=device, device_id_type=MESH)

        if when is None:
            signal()
        else:
            pl.when(when)(signal)

    for d in (1, -1, 2, -2, 3, -3, 4, -4):
        greet(at_z(d))
    for device in (up_x, down_x, up_y, down_y, partner):
        greet(device)
    for other in range(4):
        greet({"x": other, "y": x}, jnp.logical_or(x != other, y != x))
    for r in (1, 3, 2):
        for ps in range(4):
            origin = {"zh": ring(zh - r, 4), "p": ps, "c": source_core}
            upward = r == 1 or (r == 2 and ps >= 2)
            greet(origin, p == (0 if upward else 3))
    o_ref[...] = jnp.zeros_like(o_ref)
    load_d.wait()
    load_own.wait()
    load_r.wait()
    pl.semaphore_wait(
        barrier,
        4 - diagonal.astype(jnp.int32) + 8 + 5 + jnp.where(holder, 2, 4),
    )

    def go(order, inner):
        started = []

        def send(src, dst, sem, device, when=None):
            copy = pltpu.make_async_remote_copy(
                src_ref=src,
                dst_ref=dst,
                send_sem=ss.at[len(started)],
                recv_sem=sem,
                device_id=device,
                device_id_type=MESH,
            )
            started.append((copy, when))
            if when is None:
                copy.start()
            else:
                pl.when(when)(copy.start)

        def arrived(dst, sem, when=None):
            copy = pltpu.make_async_copy(dst, dst, sem)
            if when is None:
                copy.wait()
            else:
                pl.when(when)(copy.wait)

        for part in range(4):
            send(
                dv.at[pl.ds(16 * part, 16)],
                turned.at[x],
                tz.at[x],
                {"x": y, "y": part},
                jnp.logical_or(x != y, y != part),
            )

        @pl.when(diagonal)
        def _():
            turned[x] = dv[pl.ds(pl.multiple_of(16 * y, 16), 16), :]

        def turned_in():
            for other in range(4):
                arrived(
                    turned.at[other],
                    tz.at[other],
                    jnp.logical_or(x != other, y != x),
                )

        def block(core, slot, part, half=None):
            first, count = (4 * slot, 4) if half is None else (4 * slot + 2 * half, 2)
            return dbuf.at[core, pl.ds(first, count), part]

        def d_send():
            for h in range(2):
                target = 2 * c + h
                rel = ring(target - zh, 4)
                up = jnp.logical_or(rel == 1, jnp.logical_and(rel == 2, p >= 2))
                entry = jnp.where(rel == 0, p, jnp.where(up, 0, 3))
                slot = 4 * rel + p
                for core in range(2):
                    columns = pl.ds(512 * h + 256 * core, 256)
                    mine = jnp.logical_and(rel == 0, c == core)
                    send(
                        turned.at[:, :, columns],
                        block(core, slot, y),
                        dz.at[slot],
                        {"zh": target, "p": entry, "c": core},
                        jnp.logical_not(mine),
                    )

                    @pl.when(mine)
                    def _():
                        dbuf[core, pl.ds(4 * p, 4), y] = turned[:, :, columns]

        ahead, behind = at_z(jnp.where(low, 1, -1)), at_z(jnp.where(low, -1, 1))
        group_of = {
            OWN: 0,
            NEAR: jnp.where(low, 1, 3),
            AWAY: jnp.where(low, 3, 1),
            FAR: 2,
        }
        here = 1 if inner else 0

        def slot_of(r, k):
            return 4 * group_of[r] + jnp.where(low, k, 3 - k)

        def d_slot(r, k):
            slot = slot_of(r, k)
            held = block(c, slot, y)
            if r == OWN and k == here:
                arrived(held, dz.at[slot], jnp.logical_not(holder))
            else:
                arrived(held, dz.at[slot])
            if r == OWN:
                goes = (k <= here, k >= here and inner)
            elif r == NEAR or (r == FAR and k >= 2):
                goes = (True, False)
            else:
                goes = (False, inner)
            for wanted, device in zip(goes, (ahead, behind)):
                if wanted:
                    send(held, held, dz.at[slot], device)
            send(held, held, dy.at[0, slot], up_y)
            send(held, held, dy.at[1, slot], down_y)
            to_partner(r, 0)

        y_of = [y, ring(y - 1, 4), ring(y + 1, 4), ring(y + 2, 4)]
        missing = {(r, which): 4 for r in group_of for which in range(4)}

        def whole(core, r, which):
            first = pl.multiple_of(16 * group_of[r], 16)
            return dbuf.at[core, pl.ds(first, 16), y_of[which]]

        def to_partner(r, which):
            missing[r, which] -= 1
            if missing[r, which] == 0:
                part = whole(c, r, which)
                send(part, part, dd.at[group_of[r], which], partner)

        def y_relay(side, r, k):
            slot, part = slot_of(r, k), y_of[1 + side]
            arrived(block(c, slot, part), dy.at[side, slot])
            half = block(c, slot, part, side)
            send(half, half, dy.at[2 + side, slot], (up_y, down_y)[side])
            to_partner(r, 1 + side)

        def y_last(r, k):
            slot = slot_of(r, k)
            for side in range(2):
                arrived(block(c, slot, y_of[3], side), dy.at[2 + side, slot])
            to_partner(r, 3)

        def piece(number, owner, half=None):
            first, count = PIECES[number]
            if half is not None:
                first, count = first + half * (count // 2), count // 2
            return rbuf.at[owner, pl.ds(first, count)]

        def z_send(d):
            quarter = pl.ds(pl.multiple_of(ring(p + d, 4) * 256, 256), 256)
            slot = (-d) % 16
            send(rv.at[:, quarter], piece(slot, x), rz.at[slot], at_z(d))

        def z_relay(number):
            side, cut = (4, 12) if number >= 12 else (-4, 4)
            half = (1 if cut == 12 else 0) if number == cut else None
            there = {12: 16, 4: 8}.get(number, number - side)
            send(piece(number, x, half), piece(there, x), rz.at[there], at_z(side))

        def along_x(number):
            for side, device in ((0, up_x), (1, down_x)):
                send(piece(number, x), piece(number, x), rx.at[side, number], device)

        def r_slot(number):
            arrived(piece(number, x), rz.at[number])
            along_x(number)

        x_of = [ring(x - 1, 4), ring(x + 1, 4), ring(x + 2, 4)]

        def x_relay(side, number):
            arrived(piece(number, x_of[side]), rx.at[side, number])
            half = piece(number, x_of[side], side)
            send(half, half, rx.at[2 + side, number], (up_x, down_x)[side])

        def x_last(number):
            for side in range(2):
                arrived(piece(number, x_of[2], side), rx.at[2 + side, number])

        def prepare(r):
            for which in range(4):
                arrived(whole(1 - c, r, which), dd.at[group_of[r], which])

            @pl.loop(0, 4)
            def _(ps):
                slot = 4 * group_of[r] + ps
                for half in range(2):
                    value = dbuf[half, pl.ds(4 * slot, 4)].reshape(256, 256).T
                    high, rest = split(value)
                    dth[slot, pl.ds(256 * half, 256), :] = high
                    dtl[slot, pl.ds(256 * half, 256), :] = rest

        def multiply(r, k):
            slot = slot_of(r, k)
            there = ring(jnp.where(low, k, 3 - k) - p - 4 * group_of[r], 16)
            rows = pl.ds(pl.multiple_of(64 * there, 64), 64)
            high, rest = split(rbuf[:, rows, :].reshape(256, 256))
            dh, dl = dth[slot], dtl[slot]
            o_ref[...] += (
                jnp.dot(dh, high, preferred_element_type=F32)
                + jnp.dot(dl, high, preferred_element_type=F32)
                + jnp.dot(dh, rest, preferred_element_type=F32)
            )

        steps = {
            X_OWN: lambda: along_x(0),
            Z_SEND: z_send,
            TURNED: turned_in,
            D_SEND: d_send,
            D_SLOT: d_slot,
            Y_UP: lambda r, k: y_relay(0, r, k),
            Y_DOWN: lambda r, k: y_relay(1, r, k),
            Y_LAST: y_last,
            R_SLOT: r_slot,
            Z_RELAY: z_relay,
            X_UP: lambda number: x_relay(0, number),
            X_DOWN: lambda number: x_relay(1, number),
            X_LAST: x_last,
            PREPARE: prepare,
            MULTIPLY: multiply,
        }
        for name, *numbers in order:
            steps[name](*numbers)
        for copy, when in started:
            if when is None:
                copy.wait_send()
            else:
                pl.when(when)(copy.wait_send)

    edge = jnp.logical_or(p == 0, p == 3)
    pl.when(edge)(lambda: go(EDGE, False))
    pl.when(jnp.logical_not(edge))(lambda: go(INNER, True))


def body(design, responses):
    dma = pltpu.SemaphoreType.DMA
    held = [pltpu.with_memory_space_constraint(v, pltpu.HBM) for v in (design, responses)]
    return pl.pallas_call(
        kernel,
        out_shape=jax.ShapeDtypeStruct((512, 256), F32),
        in_specs=[pl.BlockSpec(memory_space=pltpu.HBM)] * 2,
        out_specs=pl.BlockSpec(memory_space=pltpu.VMEM),
        scratch_shapes=[
            pltpu.VMEM((64, 1024), F32),
            pltpu.VMEM((64, 1024), F32),
            pltpu.VMEM((4, 16, 1024), F32),
            pltpu.VMEM((2, 64, 4, 16, 256), F32),
            pltpu.VMEM((4, 1024, 256), F32),
            pltpu.VMEM((16, 512, 256), BF16),
            pltpu.VMEM((16, 512, 256), BF16),
            dma((3,)),
            dma((200,)),
            dma((4,)),
            dma((16,)),
            dma((4, 16)),
            dma((4, 4)),
            dma((17,)),
            dma((4, 17)),
        ],
        compiler_params=pltpu.CompilerParams(
            collective_id=0, has_side_effects=True, vmem_limit_bytes=32 * 2**20
        ),
    )(*held)


def solution(mesh):
    finer = Mesh(
        mesh.devices.reshape(4, 4, 4, 2, 4), ("x", "zh", "y", "c", "p")
    )
    spec = P(("x", "zh", "p"), ("y", "c"))
    return jax.shard_map(
        body,
        mesh=finer,
        in_specs=(spec, spec),
        out_specs=P(("x", "zh"), ("y", "c", "p")),
        check_vma=False,
    )
```

time: 281 us -> 96.9 us (0.34)
  waiting for transfers between devices: 159 us -> 0 us
  Pallas kernels: 0 us -> 96 us
  blocking collectives: 53.4 us -> 0 us
  starting transfers between devices: 23.5 us -> 0 us
  matrix products: 15 us -> 0 us
  local copies, waits for them, and re-layouts: 14.8 us -> 0.8 us
  between operations: 13.4 us -> 0.01 us
    all_gather x2 -> x0, waiting for transfers between devices: 133 us -> none  [gathered_by_axis(): result = lax.all_gather(result, axes[number], axis=dim, tiled=True)]
    pallas_call x0 -> x1, Pallas kernels: none -> 96 us  [body(): pl.pallas_call(kernel, out_shape=jax.ShapeDtypeStruct((512, 256), F32), i...]
    all_to_all x1 -> x0, blocking collectives: 53.4 us -> none  [summed_on_arrival(): lax.all_to_all(in_blocks(array, dim, devices), axis, 0, 0, tiled=True)]
    all_to_all x2 -> x0, waiting for transfers between devices: 25.5 us -> none  [the longest x1 25.5 us: copy_for_each(): lax.all_to_all(jnp.broadcast_to(array[None], (devices, *array.shape)), ax...]
    all_to_all x2 -> x0, starting transfers between devices: 23.4 us -> none  [the longest x1 13.1 us: body(): lax.all_to_all(widened, ROW, split_axis=1, concat_axis=0, tiled=True)]
    dot_general x1 -> x0, matrix products: 15 us -> none  [body(): lax.dot_general(design_panel, gathered_by_axis(responses, ROW, 0), (((0,)...]
    dot_general x1 -> x0, local copies, waits for them, and re-layouts: 5.37 us -> none  [body(): lax.dot_general(design_panel, gathered_by_axis(responses, ROW, 0), (((0,)...]
    all_to_all x2 -> x0, local copies, waits for them, and re-layouts: 4.32 us -> none  [body(): lax.all_to_all(widened, ROW, split_axis=1, concat_axis=0, tiled=True)]
  transfers between devices with their start and end apart: 4 -> 0, of which waited for: 3 -> 0; matrix products, arithmetic and copies ran while one was open for 4% -> 0% of each run, Pallas kernels for 0% -> 0%
where the time goes in v2:
time: 96.9 us; the launch traced here: 96.8 us
  Pallas kernels  96 us (99%)
    pallas_call x1, Pallas kernels, body(): pl.pallas_call(kernel, out_shape=jax.ShapeDtypeStruct((512, 256), F32), i...  96 us

profile of v2, /device:TPU:1, one launch (start us, length us, event | category | flops | bytes accessed | tf_op | source)
XLA Modules:
  0.0 96.8 jit_solution(6331283762668647482)
XLA Ops:
  0.0 96.0 %shard_map.28 = f32[512,256]{1,0:T(8,128)S(1)} custom-call(f32[64,1024]{1,0:T(8,128)} %d_hbm.1, f32[64,1024]{1,0:T(8,128)} %r_hbm.1), custom_call_target="tpu_custom_call" | custom-call | tf_op jit(solution)/shard_map/pallas_call | solution.py:364
  96.0 0.8 copy.4

commit v3 on v2

--- a/solution.py
+++ b/solution.py
@@ -14,56 +14,56 @@
 OWN, NEAR, AWAY, FAR = range(4)
 
 EDGE = [
-    (Z_SEND, -1), (Z_SEND, 4), (Z_SEND, 3), (Z_SEND, 1), (Z_SEND, -2), (Z_SEND, -4), (Z_SEND, -3), (Z_SEND, 2), (TURNED,),
-    (D_SEND,), (D_SLOT, OWN, 0), (R_SLOT, 14), (D_SLOT, NEAR, 1), (R_SLOT, 15), (X_UP, 14), (D_SLOT, NEAR, 0),
-    (D_SLOT, NEAR, 2), (R_SLOT, 12), (R_SLOT, 3), (Z_RELAY, 15), (R_SLOT, 2), (R_SLOT, 4), (Z_RELAY, 2), (D_SLOT, NEAR, 3),
-    (D_SLOT, FAR, 3), (X_DOWN, 12), (Z_RELAY, 14), (D_SLOT, OWN, 3), (X_DOWN, 4), (X_DOWN, 3), (Y_DOWN, NEAR, 3),
-    (R_SLOT, 1), (Y_UP, OWN, 0), (Y_UP, FAR, 3), (Y_UP, NEAR, 3), (D_SLOT, OWN, 2), (Y_DOWN, NEAR, 0), (R_SLOT, 11),
-    (Z_RELAY, 4), (X_DOWN, 14), (X_DOWN, 15), (D_SLOT, OWN, 1), (Y_DOWN, NEAR, 1), (Y_DOWN, OWN, 3), (Y_LAST, NEAR, 3),
-    (Y_DOWN, OWN, 2), (X_OWN,), (Y_UP, NEAR, 1), (R_SLOT, 13), (X_LAST, 14), (Y_UP, OWN, 2), (D_SLOT, AWAY, 2),
-    (R_SLOT, 6), (X_UP, 12), (X_DOWN, 13), (D_SLOT, AWAY, 3), (D_SLOT, FAR, 2), (X_UP, 4), (X_UP, 2), (R_SLOT, 10),
-    (Y_LAST, NEAR, 1), (Y_UP, NEAR, 0), (X_UP, 1), (Y_UP, NEAR, 2), (Z_RELAY, 12), (X_UP, 11), (Z_RELAY, 1), (X_UP, 15),
-    (Y_UP, OWN, 3), (R_SLOT, 8), (Y_DOWN, OWN, 1), (X_UP, 0), (Y_DOWN, NEAR, 2), (Y_UP, OWN, 1), (X_UP, 13),
-    (Y_LAST, OWN, 1), (Y_UP, AWAY, 2), (X_DOWN, 1), (R_SLOT, 16), (X_DOWN, 6), (X_UP, 6), (Y_DOWN, AWAY, 2),
-    (Y_DOWN, OWN, 0), (X_DOWN, 11), (D_SLOT, AWAY, 1), (Y_DOWN, AWAY, 3), (D_SLOT, AWAY, 0), (X_LAST, 12), (Z_RELAY, 13),
-    (Y_LAST, NEAR, 0), (X_DOWN, 0), (Y_LAST, NEAR, 2), (R_SLOT, 5), (PREPARE, NEAR), (X_LAST, 1), (Y_DOWN, FAR, 2),
-    (X_UP, 10), (X_DOWN, 2), (Z_RELAY, 3), (D_SLOT, FAR, 0), (Y_DOWN, AWAY, 0), (Y_LAST, OWN, 2), (X_LAST, 15),
-    (X_DOWN, 10), (X_UP, 3), (Y_UP, AWAY, 3), (X_LAST, 13), (Y_UP, FAR, 2), (R_SLOT, 9), (Y_UP, AWAY, 1), (Y_DOWN, FAR, 3),
-    (X_UP, 5), (Y_DOWN, AWAY, 1), (X_DOWN, 5), (X_LAST, 0), (Y_UP, AWAY, 0), (X_LAST, 2), (X_LAST, 4), (Y_LAST, AWAY, 2),
-    (X_UP, 16), (X_DOWN, 16), (X_LAST, 3), (Y_LAST, OWN, 3), (D_SLOT, FAR, 1), (X_UP, 8), (Y_LAST, AWAY, 3), (X_DOWN, 8),
-    (Y_LAST, OWN, 0), (Y_DOWN, FAR, 0), (MULTIPLY, NEAR, 2), (X_LAST, 10), (Y_UP, FAR, 0), (R_SLOT, 7), (PREPARE, OWN),
-    (X_UP, 9), (Y_UP, FAR, 1), (Y_DOWN, FAR, 1), (Y_LAST, FAR, 3), (X_DOWN, 9), (MULTIPLY, OWN, 2), (MULTIPLY, OWN, 0),
-    (Y_LAST, AWAY, 1), (Y_LAST, FAR, 2), (MULTIPLY, OWN, 3), (Y_LAST, FAR, 0), (Y_LAST, AWAY, 0), (X_LAST, 16),
-    (X_LAST, 11), (X_LAST, 6), (X_LAST, 5), (MULTIPLY, NEAR, 0), (MULTIPLY, NEAR, 3), (X_UP, 7), (X_DOWN, 7),
-    (MULTIPLY, NEAR, 1), (MULTIPLY, OWN, 1), (Y_LAST, FAR, 1), (X_LAST, 8), (PREPARE, AWAY), (MULTIPLY, AWAY, 0),
-    (PREPARE, FAR), (X_LAST, 7), (X_LAST, 9), (MULTIPLY, AWAY, 3), (MULTIPLY, AWAY, 1), (MULTIPLY, FAR, 1),
-    (MULTIPLY, FAR, 2), (MULTIPLY, FAR, 3), (MULTIPLY, FAR, 0), (MULTIPLY, AWAY, 2),
+    (Z_SEND, -1), (Z_SEND, 4), (Z_SEND, 3), (Z_SEND, -2), (Z_SEND, 2), (Z_SEND, 1), (Z_SEND, -4), (Z_SEND, -3), (TURNED,),
+    (D_SEND,), (R_SLOT, 3), (D_SLOT, OWN, 0), (R_SLOT, 1), (D_SLOT, NEAR, 1), (R_SLOT, 15), (R_SLOT, 2), (R_SLOT, 12),
+    (R_SLOT, 14), (X_UP, 1), (D_SLOT, NEAR, 0), (R_SLOT, 4), (D_SLOT, NEAR, 3), (Z_RELAY, 4), (D_SLOT, NEAR, 2),
+    (D_SLOT, FAR, 3), (Z_RELAY, 15), (Z_RELAY, 14), (Y_UP, NEAR, 1), (Y_UP, NEAR, 2), (X_UP, 14), (Y_DOWN, NEAR, 2),
+    (X_DOWN, 1), (X_UP, 12), (Z_RELAY, 2), (X_UP, 2), (Y_DOWN, OWN, 0), (D_SLOT, OWN, 2), (X_DOWN, 4), (Y_LAST, NEAR, 2),
+    (Y_DOWN, NEAR, 1), (X_DOWN, 2), (D_SLOT, AWAY, 2), (Y_DOWN, OWN, 2), (X_LAST, 1), (R_SLOT, 8), (R_SLOT, 6),
+    (Y_DOWN, FAR, 3), (Y_UP, NEAR, 0), (X_DOWN, 12), (D_SLOT, FAR, 2), (D_SLOT, OWN, 3), (X_OWN,), (R_SLOT, 11),
+    (Y_UP, AWAY, 2), (X_UP, 8), (Y_UP, NEAR, 3), (Y_DOWN, AWAY, 2), (X_DOWN, 14), (Y_UP, OWN, 2), (R_SLOT, 13),
+    (R_SLOT, 10), (Y_UP, FAR, 3), (X_UP, 3), (Y_DOWN, NEAR, 3), (D_SLOT, OWN, 1), (Z_RELAY, 12), (X_DOWN, 0), (X_DOWN, 3),
+    (D_SLOT, AWAY, 3), (Z_RELAY, 13), (Y_DOWN, NEAR, 0), (Y_UP, OWN, 1), (X_LAST, 14), (Y_UP, FAR, 2), (X_DOWN, 6),
+    (X_UP, 11), (R_SLOT, 16), (D_SLOT, AWAY, 0), (Y_LAST, NEAR, 3), (X_DOWN, 13), (X_UP, 0), (X_UP, 10), (X_DOWN, 11),
+    (X_UP, 4), (Y_DOWN, OWN, 3), (X_DOWN, 8), (X_UP, 6), (X_UP, 13), (Y_UP, OWN, 0), (Y_LAST, NEAR, 0), (Y_DOWN, OWN, 1),
+    (X_DOWN, 15), (Y_UP, OWN, 3), (Z_RELAY, 1), (X_LAST, 12), (Y_DOWN, AWAY, 3), (Y_LAST, NEAR, 1), (PREPARE, NEAR),
+    (Z_RELAY, 3), (X_LAST, 3), (X_UP, 15), (X_LAST, 2), (X_DOWN, 10), (Y_DOWN, FAR, 2), (D_SLOT, AWAY, 1),
+    (Y_LAST, OWN, 1), (Y_LAST, OWN, 2), (Y_UP, AWAY, 0), (D_SLOT, FAR, 0), (Y_UP, AWAY, 3), (X_LAST, 0), (R_SLOT, 5),
+    (Y_LAST, FAR, 3), (Y_LAST, OWN, 0), (Y_LAST, FAR, 2), (X_UP, 16), (Y_DOWN, AWAY, 1), (X_DOWN, 16), (Y_LAST, AWAY, 2),
+    (R_SLOT, 9), (Y_DOWN, AWAY, 0), (X_LAST, 15), (D_SLOT, FAR, 1), (Y_LAST, OWN, 3), (X_LAST, 13), (MULTIPLY, NEAR, 3),
+    (Y_UP, FAR, 0), (Y_UP, AWAY, 1), (Y_DOWN, FAR, 0), (X_LAST, 11), (X_DOWN, 5), (X_LAST, 6), (X_UP, 5), (R_SLOT, 7),
+    (PREPARE, OWN), (MULTIPLY, OWN, 3), (Y_LAST, AWAY, 3), (Y_LAST, AWAY, 0), (MULTIPLY, OWN, 0), (Y_DOWN, FAR, 1),
+    (Y_UP, FAR, 1), (MULTIPLY, OWN, 1), (Y_LAST, FAR, 0), (X_LAST, 8), (Y_LAST, AWAY, 1), (MULTIPLY, OWN, 2), (X_UP, 7),
+    (X_DOWN, 9), (X_LAST, 5), (PREPARE, AWAY), (X_UP, 9), (X_LAST, 4), (X_DOWN, 7), (MULTIPLY, AWAY, 0),
+    (MULTIPLY, AWAY, 1), (Y_LAST, FAR, 1), (X_LAST, 10), (MULTIPLY, NEAR, 2), (MULTIPLY, AWAY, 2), (MULTIPLY, NEAR, 0),
+    (PREPARE, FAR), (MULTIPLY, FAR, 3), (MULTIPLY, NEAR, 1), (X_LAST, 9), (X_LAST, 7), (X_LAST, 16), (MULTIPLY, FAR, 2),
+    (MULTIPLY, AWAY, 3), (MULTIPLY, FAR, 0), (MULTIPLY, FAR, 1),
 ]
 INNER = [
-    (Z_SEND, -1), (Z_SEND, 4), (Z_SEND, -2), (Z_SEND, 3), (Z_SEND, -4), (Z_SEND, 2), (Z_SEND, 1), (Z_SEND, -3), (TURNED,),
-    (D_SEND,), (X_OWN,), (D_SLOT, OWN, 1), (D_SLOT, OWN, 0), (D_SLOT, OWN, 2), (R_SLOT, 4), (R_SLOT, 14),
-    (D_SLOT, NEAR, 1), (D_SLOT, NEAR, 0), (R_SLOT, 15), (D_SLOT, OWN, 3), (D_SLOT, NEAR, 2), (R_SLOT, 1), (Y_DOWN, OWN, 2),
-    (X_DOWN, 0), (D_SLOT, AWAY, 2), (R_SLOT, 2), (D_SLOT, AWAY, 3), (Y_DOWN, OWN, 0), (X_UP, 14), (D_SLOT, NEAR, 3),
-    (Z_RELAY, 1), (Y_UP, OWN, 1), (R_SLOT, 13), (Y_UP, OWN, 0), (Y_DOWN, NEAR, 2), (X_DOWN, 2), (Z_RELAY, 2),
-    (Y_UP, NEAR, 0), (X_UP, 15), (R_SLOT, 12), (Z_RELAY, 14), (X_DOWN, 15), (R_SLOT, 3), (Y_LAST, OWN, 0), (Y_UP, NEAR, 2),
-    (D_SLOT, AWAY, 1), (X_DOWN, 1), (X_UP, 0), (Y_DOWN, NEAR, 0), (Z_RELAY, 15), (X_UP, 3), (Y_UP, OWN, 2), (R_SLOT, 10),
-    (D_SLOT, AWAY, 0), (D_SLOT, FAR, 3), (Z_RELAY, 12), (X_DOWN, 12), (Y_DOWN, NEAR, 3), (R_SLOT, 5), (Z_RELAY, 3),
-    (Y_DOWN, AWAY, 0), (X_DOWN, 14), (Y_DOWN, AWAY, 2), (Y_UP, NEAR, 3), (Y_UP, AWAY, 0), (X_UP, 1), (X_DOWN, 3),
-    (Y_DOWN, OWN, 3), (Y_UP, AWAY, 2), (X_UP, 4), (Y_LAST, NEAR, 0), (X_DOWN, 10), (X_UP, 13), (Y_DOWN, NEAR, 1),
-    (X_LAST, 0), (X_DOWN, 4), (Z_RELAY, 4), (X_UP, 5), (D_SLOT, FAR, 0), (R_SLOT, 6), (X_DOWN, 13), (D_SLOT, FAR, 2),
-    (X_UP, 12), (Y_UP, AWAY, 1), (R_SLOT, 11), (Y_UP, NEAR, 1), (Y_LAST, AWAY, 2), (X_UP, 6), (Y_DOWN, OWN, 1),
-    (Y_UP, AWAY, 3), (Y_LAST, NEAR, 2), (X_LAST, 14), (Y_DOWN, FAR, 0), (R_SLOT, 7), (X_LAST, 1), (Z_RELAY, 13),
-    (Y_LAST, OWN, 2), (X_DOWN, 5), (X_LAST, 12), (Y_LAST, NEAR, 3), (D_SLOT, FAR, 1), (R_SLOT, 8), (X_UP, 2),
-    (Y_DOWN, AWAY, 3), (X_UP, 10), (R_SLOT, 16), (Y_LAST, NEAR, 1), (Y_UP, OWN, 3), (Y_LAST, OWN, 1), (X_DOWN, 11),
-    (X_UP, 7), (X_DOWN, 7), (X_LAST, 3), (Y_DOWN, AWAY, 1), (X_LAST, 4), (Y_LAST, AWAY, 0), (X_LAST, 13), (PREPARE, NEAR),
-    (X_LAST, 2), (X_UP, 11), (X_UP, 16), (Y_UP, FAR, 1), (Y_LAST, AWAY, 3), (Y_LAST, OWN, 3), (Y_UP, FAR, 0), (X_DOWN, 6),
-    (MULTIPLY, NEAR, 2), (R_SLOT, 9), (X_LAST, 7), (Y_DOWN, FAR, 3), (X_LAST, 15), (X_DOWN, 16), (MULTIPLY, NEAR, 1),
-    (X_LAST, 5), (PREPARE, OWN), (Y_DOWN, FAR, 1), (X_UP, 8), (Y_LAST, AWAY, 1), (Y_UP, FAR, 3), (Y_DOWN, FAR, 2),
-    (MULTIPLY, OWN, 0), (X_DOWN, 8), (Y_LAST, FAR, 0), (Y_UP, FAR, 2), (X_DOWN, 9), (X_UP, 9), (MULTIPLY, OWN, 3),
-    (MULTIPLY, OWN, 1), (X_LAST, 10), (MULTIPLY, NEAR, 3), (X_LAST, 11), (MULTIPLY, OWN, 2), (PREPARE, AWAY),
-    (Y_LAST, FAR, 3), (MULTIPLY, AWAY, 0), (X_LAST, 16), (MULTIPLY, AWAY, 1), (X_LAST, 6), (X_LAST, 8), (Y_LAST, FAR, 1),
-    (X_LAST, 9), (Y_LAST, FAR, 2), (MULTIPLY, AWAY, 3), (MULTIPLY, AWAY, 2), (MULTIPLY, NEAR, 0), (PREPARE, FAR),
-    (MULTIPLY, FAR, 3), (MULTIPLY, FAR, 0), (MULTIPLY, FAR, 2), (MULTIPLY, FAR, 1),
+    (Z_SEND, 4), (Z_SEND, 3), (Z_SEND, -1), (Z_SEND, -2), (Z_SEND, 1), (Z_SEND, 2), (Z_SEND, -4), (Z_SEND, -3), (TURNED,),
+    (D_SEND,), (R_SLOT, 14), (R_SLOT, 1), (D_SLOT, OWN, 1), (X_UP, 1), (D_SLOT, OWN, 2), (R_SLOT, 15), (D_SLOT, OWN, 0),
+    (D_SLOT, NEAR, 1), (R_SLOT, 12), (D_SLOT, NEAR, 0), (Y_DOWN, OWN, 2), (D_SLOT, NEAR, 3), (Y_UP, OWN, 0),
+    (D_SLOT, OWN, 3), (R_SLOT, 3), (Y_DOWN, OWN, 1), (Y_UP, OWN, 2), (R_SLOT, 4), (R_SLOT, 2), (X_DOWN, 12),
+    (D_SLOT, AWAY, 2), (X_UP, 12), (X_DOWN, 1), (X_UP, 4), (Y_DOWN, NEAR, 0), (X_DOWN, 14), (D_SLOT, NEAR, 2), (X_DOWN, 3),
+    (Z_RELAY, 2), (Z_RELAY, 1), (X_OWN,), (Z_RELAY, 14), (D_SLOT, AWAY, 3), (Z_RELAY, 3), (X_UP, 14), (Y_UP, NEAR, 0),
+    (Y_DOWN, NEAR, 2), (X_DOWN, 4), (R_SLOT, 13), (X_DOWN, 0), (Y_UP, NEAR, 2), (Z_RELAY, 15), (Y_DOWN, OWN, 3),
+    (Y_DOWN, AWAY, 3), (D_SLOT, FAR, 3), (R_SLOT, 6), (X_LAST, 1), (Y_LAST, NEAR, 2), (D_SLOT, AWAY, 0), (Y_UP, OWN, 1),
+    (X_DOWN, 2), (D_SLOT, AWAY, 1), (R_SLOT, 5), (D_SLOT, FAR, 2), (Z_RELAY, 4), (Y_DOWN, OWN, 0), (Y_UP, OWN, 3),
+    (Z_RELAY, 12), (X_UP, 13), (Y_DOWN, AWAY, 0), (X_UP, 15), (Y_UP, AWAY, 0), (X_UP, 3), (Y_DOWN, NEAR, 3),
+    (D_SLOT, FAR, 0), (Y_DOWN, FAR, 3), (R_SLOT, 11), (X_UP, 6), (Y_UP, AWAY, 1), (Y_UP, FAR, 3), (Y_DOWN, FAR, 2),
+    (Y_UP, NEAR, 1), (Y_UP, NEAR, 3), (X_LAST, 12), (Z_RELAY, 13), (Y_DOWN, NEAR, 1), (X_UP, 2), (R_SLOT, 10),
+    (X_DOWN, 15), (R_SLOT, 7), (Y_UP, FAR, 2), (Y_DOWN, FAR, 0), (X_DOWN, 13), (R_SLOT, 8), (D_SLOT, FAR, 1),
+    (Y_DOWN, AWAY, 1), (X_UP, 11), (X_DOWN, 5), (Y_LAST, OWN, 1), (X_UP, 0), (X_DOWN, 11), (X_LAST, 4), (Y_UP, FAR, 0),
+    (Y_UP, AWAY, 3), (Y_LAST, OWN, 3), (Y_LAST, FAR, 3), (Y_LAST, NEAR, 1), (Y_DOWN, AWAY, 2), (X_DOWN, 6),
+    (Y_LAST, FAR, 0), (X_DOWN, 7), (R_SLOT, 16), (X_UP, 10), (Y_LAST, OWN, 0), (X_LAST, 13), (Y_DOWN, FAR, 1), (X_UP, 8),
+    (Y_UP, AWAY, 2), (Y_LAST, OWN, 2), (Y_LAST, AWAY, 0), (Y_UP, FAR, 1), (R_SLOT, 9), (X_LAST, 15), (Y_LAST, AWAY, 1),
+    (Y_LAST, NEAR, 3), (PREPARE, OWN), (X_LAST, 2), (X_LAST, 11), (X_LAST, 3), (X_UP, 5), (Y_LAST, FAR, 2), (X_LAST, 0),
+    (X_UP, 7), (Y_LAST, NEAR, 0), (X_DOWN, 10), (Y_LAST, AWAY, 2), (Y_LAST, AWAY, 3), (X_LAST, 14), (MULTIPLY, OWN, 2),
+    (PREPARE, NEAR), (Y_LAST, FAR, 1), (MULTIPLY, OWN, 3), (X_UP, 9), (X_DOWN, 8), (X_UP, 16), (X_DOWN, 9),
+    (MULTIPLY, NEAR, 2), (MULTIPLY, NEAR, 1), (X_DOWN, 16), (X_LAST, 5), (PREPARE, AWAY), (PREPARE, FAR), (X_LAST, 10),
+    (MULTIPLY, AWAY, 0), (X_LAST, 7), (MULTIPLY, NEAR, 0), (X_LAST, 8), (X_LAST, 6), (MULTIPLY, OWN, 1), (X_LAST, 9),
+    (MULTIPLY, AWAY, 2), (X_LAST, 16), (MULTIPLY, FAR, 0), (MULTIPLY, FAR, 3), (MULTIPLY, AWAY, 3), (MULTIPLY, FAR, 1),
+    (MULTIPLY, OWN, 0), (MULTIPLY, NEAR, 3), (MULTIPLY, AWAY, 1), (MULTIPLY, FAR, 2),
 ]
 
 PIECES = (

time: 96.9 us -> 93.9 us (0.969)
  Pallas kernels: 96 us -> 92.4 us
    pallas_call x1, Pallas kernels: 96 us -> 92.4 us  [body(): pl.pallas_call(kernel, out_shape=jax.ShapeDtypeStruct((512, 256), F32), i...]
where the time goes in v3:
time: 93.9 us; the launch traced here: 93.2 us
  Pallas kernels  92.4 us (98%)
    pallas_call x1, Pallas kernels, body(): pl.pallas_call(kernel, out_shape=jax.ShapeDtypeStruct((512, 256), F32), i...  92.4 us

profile of v3, /device:TPU:1, one launch (start us, length us, event | category | flops | bytes accessed | tf_op | source)
XLA Modules:
  0.0 93.2 jit_solution(601723297260896579)
XLA Ops:
  0.0 92.4 %shard_map.28 = f32[512,256]{1,0:T(8,128)S(1)} custom-call(f32[64,1024]{1,0:T(8,128)} %d_hbm.1, f32[64,1024]{1,0:T(8,128)} %r_hbm.1), custom_call_target="tpu_custom_call" | custom-call | tf_op jit(solution)/shard_map/pallas_call | solution.py:364
  92.4 0.8 copy.4

commit v4 on v3

--- a/solution.py
+++ b/solution.py
@@ -14,56 +14,56 @@
 OWN, NEAR, AWAY, FAR = range(4)
 
 EDGE = [
-    (Z_SEND, -1), (Z_SEND, 4), (Z_SEND, 3), (Z_SEND, -2), (Z_SEND, 2), (Z_SEND, 1), (Z_SEND, -4), (Z_SEND, -3), (TURNED,),
-    (D_SEND,), (R_SLOT, 3), (D_SLOT, OWN, 0), (R_SLOT, 1), (D_SLOT, NEAR, 1), (R_SLOT, 15), (R_SLOT, 2), (R_SLOT, 12),
-    (R_SLOT, 14), (X_UP, 1), (D_SLOT, NEAR, 0), (R_SLOT, 4), (D_SLOT, NEAR, 3), (Z_RELAY, 4), (D_SLOT, NEAR, 2),
-    (D_SLOT, FAR, 3), (Z_RELAY, 15), (Z_RELAY, 14), (Y_UP, NEAR, 1), (Y_UP, NEAR, 2), (X_UP, 14), (Y_DOWN, NEAR, 2),
-    (X_DOWN, 1), (X_UP, 12), (Z_RELAY, 2), (X_UP, 2), (Y_DOWN, OWN, 0), (D_SLOT, OWN, 2), (X_DOWN, 4), (Y_LAST, NEAR, 2),
-    (Y_DOWN, NEAR, 1), (X_DOWN, 2), (D_SLOT, AWAY, 2), (Y_DOWN, OWN, 2), (X_LAST, 1), (R_SLOT, 8), (R_SLOT, 6),
-    (Y_DOWN, FAR, 3), (Y_UP, NEAR, 0), (X_DOWN, 12), (D_SLOT, FAR, 2), (D_SLOT, OWN, 3), (X_OWN,), (R_SLOT, 11),
-    (Y_UP, AWAY, 2), (X_UP, 8), (Y_UP, NEAR, 3), (Y_DOWN, AWAY, 2), (X_DOWN, 14), (Y_UP, OWN, 2), (R_SLOT, 13),
-    (R_SLOT, 10), (Y_UP, FAR, 3), (X_UP, 3), (Y_DOWN, NEAR, 3), (D_SLOT, OWN, 1), (Z_RELAY, 12), (X_DOWN, 0), (X_DOWN, 3),
-    (D_SLOT, AWAY, 3), (Z_RELAY, 13), (Y_DOWN, NEAR, 0), (Y_UP, OWN, 1), (X_LAST, 14), (Y_UP, FAR, 2), (X_DOWN, 6),
-    (X_UP, 11), (R_SLOT, 16), (D_SLOT, AWAY, 0), (Y_LAST, NEAR, 3), (X_DOWN, 13), (X_UP, 0), (X_UP, 10), (X_DOWN, 11),
-    (X_UP, 4), (Y_DOWN, OWN, 3), (X_DOWN, 8), (X_UP, 6), (X_UP, 13), (Y_UP, OWN, 0), (Y_LAST, NEAR, 0), (Y_DOWN, OWN, 1),
-    (X_DOWN, 15), (Y_UP, OWN, 3), (Z_RELAY, 1), (X_LAST, 12), (Y_DOWN, AWAY, 3), (Y_LAST, NEAR, 1), (PREPARE, NEAR),
-    (Z_RELAY, 3), (X_LAST, 3), (X_UP, 15), (X_LAST, 2), (X_DOWN, 10), (Y_DOWN, FAR, 2), (D_SLOT, AWAY, 1),
-    (Y_LAST, OWN, 1), (Y_LAST, OWN, 2), (Y_UP, AWAY, 0), (D_SLOT, FAR, 0), (Y_UP, AWAY, 3), (X_LAST, 0), (R_SLOT, 5),
-    (Y_LAST, FAR, 3), (Y_LAST, OWN, 0), (Y_LAST, FAR, 2), (X_UP, 16), (Y_DOWN, AWAY, 1), (X_DOWN, 16), (Y_LAST, AWAY, 2),
-    (R_SLOT, 9), (Y_DOWN, AWAY, 0), (X_LAST, 15), (D_SLOT, FAR, 1), (Y_LAST, OWN, 3), (X_LAST, 13), (MULTIPLY, NEAR, 3),
-    (Y_UP, FAR, 0), (Y_UP, AWAY, 1), (Y_DOWN, FAR, 0), (X_LAST, 11), (X_DOWN, 5), (X_LAST, 6), (X_UP, 5), (R_SLOT, 7),
-    (PREPARE, OWN), (MULTIPLY, OWN, 3), (Y_LAST, AWAY, 3), (Y_LAST, AWAY, 0), (MULTIPLY, OWN, 0), (Y_DOWN, FAR, 1),
-    (Y_UP, FAR, 1), (MULTIPLY, OWN, 1), (Y_LAST, FAR, 0), (X_LAST, 8), (Y_LAST, AWAY, 1), (MULTIPLY, OWN, 2), (X_UP, 7),
-    (X_DOWN, 9), (X_LAST, 5), (PREPARE, AWAY), (X_UP, 9), (X_LAST, 4), (X_DOWN, 7), (MULTIPLY, AWAY, 0),
-    (MULTIPLY, AWAY, 1), (Y_LAST, FAR, 1), (X_LAST, 10), (MULTIPLY, NEAR, 2), (MULTIPLY, AWAY, 2), (MULTIPLY, NEAR, 0),
-    (PREPARE, FAR), (MULTIPLY, FAR, 3), (MULTIPLY, NEAR, 1), (X_LAST, 9), (X_LAST, 7), (X_LAST, 16), (MULTIPLY, FAR, 2),
-    (MULTIPLY, AWAY, 3), (MULTIPLY, FAR, 0), (MULTIPLY, FAR, 1),
+    (Z_SEND, 4), (Z_SEND, 3), (Z_SEND, -1), (Z_SEND, 1), (Z_SEND, -2), (Z_SEND, -4), (Z_SEND, 2), (Z_SEND, -3), (TURNED,),
+    (D_SEND,), (R_SLOT, 12), (D_SLOT, OWN, 0), (R_SLOT, 1), (X_DOWN, 12), (X_UP, 12), (D_SLOT, NEAR, 1), (R_SLOT, 14),
+    (D_SLOT, NEAR, 0), (Y_UP, NEAR, 1), (R_SLOT, 13), (D_SLOT, NEAR, 3), (R_SLOT, 4), (D_SLOT, NEAR, 2), (X_DOWN, 1),
+    (Y_UP, NEAR, 0), (R_SLOT, 15), (R_SLOT, 2), (Z_RELAY, 15), (Z_RELAY, 4), (Z_RELAY, 14), (R_SLOT, 3), (X_UP, 15),
+    (D_SLOT, FAR, 3), (X_OWN,), (Z_RELAY, 2), (Y_UP, NEAR, 2), (Y_DOWN, NEAR, 0), (Y_DOWN, NEAR, 2), (D_SLOT, OWN, 3),
+    (X_DOWN, 15), (D_SLOT, OWN, 2), (X_UP, 3), (D_SLOT, FAR, 2), (X_DOWN, 14), (R_SLOT, 6), (D_SLOT, AWAY, 2),
+    (Y_LAST, NEAR, 2), (Y_UP, FAR, 2), (R_SLOT, 10), (Y_DOWN, OWN, 0), (Y_UP, OWN, 2), (R_SLOT, 8), (X_UP, 6),
+    (Y_DOWN, NEAR, 3), (R_SLOT, 11), (Y_UP, OWN, 0), (Y_UP, AWAY, 2), (Z_RELAY, 12), (Y_DOWN, AWAY, 2), (Y_UP, NEAR, 3),
+    (D_SLOT, OWN, 1), (Y_DOWN, OWN, 2), (Y_UP, FAR, 3), (Y_DOWN, NEAR, 1), (Y_DOWN, FAR, 3), (X_UP, 4), (Y_LAST, NEAR, 0),
+    (X_DOWN, 3), (X_UP, 11), (R_SLOT, 16), (Y_LAST, NEAR, 3), (Z_RELAY, 13), (X_UP, 0), (Y_LAST, NEAR, 1), (X_DOWN, 11),
+    (Y_UP, OWN, 3), (X_DOWN, 0), (X_DOWN, 10), (Y_LAST, OWN, 0), (X_UP, 1), (Y_DOWN, OWN, 1), (X_UP, 2), (Y_LAST, OWN, 2),
+    (D_SLOT, AWAY, 3), (X_DOWN, 6), (Y_DOWN, FAR, 2), (X_UP, 10), (Y_DOWN, OWN, 3), (D_SLOT, AWAY, 0), (Z_RELAY, 1),
+    (X_DOWN, 13), (X_UP, 13), (D_SLOT, AWAY, 1), (X_DOWN, 2), (X_LAST, 3), (X_DOWN, 8), (X_UP, 8), (X_LAST, 12),
+    (Y_UP, AWAY, 0), (X_LAST, 0), (PREPARE, NEAR), (Z_RELAY, 3), (X_LAST, 2), (X_LAST, 8), (X_LAST, 11), (X_UP, 16),
+    (Y_DOWN, AWAY, 3), (Y_DOWN, AWAY, 0), (Y_LAST, AWAY, 2), (X_DOWN, 16), (R_SLOT, 5), (Y_UP, OWN, 1), (Y_UP, AWAY, 3),
+    (X_LAST, 15), (X_UP, 14), (D_SLOT, FAR, 0), (R_SLOT, 9), (Y_DOWN, AWAY, 1), (Y_UP, AWAY, 1), (D_SLOT, FAR, 1),
+    (Y_DOWN, FAR, 0), (X_LAST, 14), (Y_LAST, OWN, 1), (R_SLOT, 7), (Y_LAST, AWAY, 3), (Y_LAST, OWN, 3), (X_LAST, 10),
+    (X_LAST, 6), (X_LAST, 16), (X_LAST, 1), (X_UP, 5), (Y_UP, FAR, 0), (X_DOWN, 5), (X_DOWN, 4), (MULTIPLY, NEAR, 3),
+    (X_DOWN, 9), (Y_LAST, AWAY, 1), (X_UP, 9), (Y_LAST, AWAY, 0), (Y_LAST, FAR, 2), (PREPARE, OWN), (Y_LAST, FAR, 3),
+    (Y_UP, FAR, 1), (Y_DOWN, FAR, 1), (MULTIPLY, OWN, 0), (PREPARE, AWAY), (X_LAST, 13), (MULTIPLY, OWN, 2), (X_LAST, 4),
+    (X_UP, 7), (X_LAST, 5), (X_DOWN, 7), (MULTIPLY, NEAR, 2), (MULTIPLY, NEAR, 1), (MULTIPLY, NEAR, 0), (Y_LAST, FAR, 0),
+    (MULTIPLY, AWAY, 2), (X_LAST, 9), (Y_LAST, FAR, 1), (MULTIPLY, OWN, 1), (MULTIPLY, AWAY, 0), (MULTIPLY, OWN, 3),
+    (PREPARE, FAR), (X_LAST, 7), (MULTIPLY, FAR, 3), (MULTIPLY, AWAY, 1), (MULTIPLY, FAR, 1), (MULTIPLY, AWAY, 3),
+    (MULTIPLY, FAR, 0), (MULTIPLY, FAR, 2),
 ]
 INNER = [
-    (Z_SEND, 4), (Z_SEND, 3), (Z_SEND, -1), (Z_SEND, -2), (Z_SEND, 1), (Z_SEND, 2), (Z_SEND, -4), (Z_SEND, -3), (TURNED,),
-    (D_SEND,), (R_SLOT, 14), (R_SLOT, 1), (D_SLOT, OWN, 1), (X_UP, 1), (D_SLOT, OWN, 2), (R_SLOT, 15), (D_SLOT, OWN, 0),
-    (D_SLOT, NEAR, 1), (R_SLOT, 12), (D_SLOT, NEAR, 0), (Y_DOWN, OWN, 2), (D_SLOT, NEAR, 3), (Y_UP, OWN, 0),
-    (D_SLOT, OWN, 3), (R_SLOT, 3), (Y_DOWN, OWN, 1), (Y_UP, OWN, 2), (R_SLOT, 4), (R_SLOT, 2), (X_DOWN, 12),
-    (D_SLOT, AWAY, 2), (X_UP, 12), (X_DOWN, 1), (X_UP, 4), (Y_DOWN, NEAR, 0), (X_DOWN, 14), (D_SLOT, NEAR, 2), (X_DOWN, 3),
-    (Z_RELAY, 2), (Z_RELAY, 1), (X_OWN,), (Z_RELAY, 14), (D_SLOT, AWAY, 3), (Z_RELAY, 3), (X_UP, 14), (Y_UP, NEAR, 0),
-    (Y_DOWN, NEAR, 2), (X_DOWN, 4), (R_SLOT, 13), (X_DOWN, 0), (Y_UP, NEAR, 2), (Z_RELAY, 15), (Y_DOWN, OWN, 3),
-    (Y_DOWN, AWAY, 3), (D_SLOT, FAR, 3), (R_SLOT, 6), (X_LAST, 1), (Y_LAST, NEAR, 2), (D_SLOT, AWAY, 0), (Y_UP, OWN, 1),
-    (X_DOWN, 2), (D_SLOT, AWAY, 1), (R_SLOT, 5), (D_SLOT, FAR, 2), (Z_RELAY, 4), (Y_DOWN, OWN, 0), (Y_UP, OWN, 3),
-    (Z_RELAY, 12), (X_UP, 13), (Y_DOWN, AWAY, 0), (X_UP, 15), (Y_UP, AWAY, 0), (X_UP, 3), (Y_DOWN, NEAR, 3),
-    (D_SLOT, FAR, 0), (Y_DOWN, FAR, 3), (R_SLOT, 11), (X_UP, 6), (Y_UP, AWAY, 1), (Y_UP, FAR, 3), (Y_DOWN, FAR, 2),
-    (Y_UP, NEAR, 1), (Y_UP, NEAR, 3), (X_LAST, 12), (Z_RELAY, 13), (Y_DOWN, NEAR, 1), (X_UP, 2), (R_SLOT, 10),
-    (X_DOWN, 15), (R_SLOT, 7), (Y_UP, FAR, 2), (Y_DOWN, FAR, 0), (X_DOWN, 13), (R_SLOT, 8), (D_SLOT, FAR, 1),
-    (Y_DOWN, AWAY, 1), (X_UP, 11), (X_DOWN, 5), (Y_LAST, OWN, 1), (X_UP, 0), (X_DOWN, 11), (X_LAST, 4), (Y_UP, FAR, 0),
-    (Y_UP, AWAY, 3), (Y_LAST, OWN, 3), (Y_LAST, FAR, 3), (Y_LAST, NEAR, 1), (Y_DOWN, AWAY, 2), (X_DOWN, 6),
-    (Y_LAST, FAR, 0), (X_DOWN, 7), (R_SLOT, 16), (X_UP, 10), (Y_LAST, OWN, 0), (X_LAST, 13), (Y_DOWN, FAR, 1), (X_UP, 8),
-    (Y_UP, AWAY, 2), (Y_LAST, OWN, 2), (Y_LAST, AWAY, 0), (Y_UP, FAR, 1), (R_SLOT, 9), (X_LAST, 15), (Y_LAST, AWAY, 1),
-    (Y_LAST, NEAR, 3), (PREPARE, OWN), (X_LAST, 2), (X_LAST, 11), (X_LAST, 3), (X_UP, 5), (Y_LAST, FAR, 2), (X_LAST, 0),
-    (X_UP, 7), (Y_LAST, NEAR, 0), (X_DOWN, 10), (Y_LAST, AWAY, 2), (Y_LAST, AWAY, 3), (X_LAST, 14), (MULTIPLY, OWN, 2),
-    (PREPARE, NEAR), (Y_LAST, FAR, 1), (MULTIPLY, OWN, 3), (X_UP, 9), (X_DOWN, 8), (X_UP, 16), (X_DOWN, 9),
-    (MULTIPLY, NEAR, 2), (MULTIPLY, NEAR, 1), (X_DOWN, 16), (X_LAST, 5), (PREPARE, AWAY), (PREPARE, FAR), (X_LAST, 10),
-    (MULTIPLY, AWAY, 0), (X_LAST, 7), (MULTIPLY, NEAR, 0), (X_LAST, 8), (X_LAST, 6), (MULTIPLY, OWN, 1), (X_LAST, 9),
-    (MULTIPLY, AWAY, 2), (X_LAST, 16), (MULTIPLY, FAR, 0), (MULTIPLY, FAR, 3), (MULTIPLY, AWAY, 3), (MULTIPLY, FAR, 1),
-    (MULTIPLY, OWN, 0), (MULTIPLY, NEAR, 3), (MULTIPLY, AWAY, 1), (MULTIPLY, FAR, 2),
+    (Z_SEND, 4), (Z_SEND, 3), (Z_SEND, -1), (Z_SEND, -2), (Z_SEND, -4), (Z_SEND, 1), (Z_SEND, 2), (Z_SEND, -3), (TURNED,),
+    (D_SEND,), (D_SLOT, OWN, 1), (D_SLOT, OWN, 2), (D_SLOT, OWN, 0), (R_SLOT, 12), (D_SLOT, NEAR, 1), (R_SLOT, 2),
+    (R_SLOT, 14), (R_SLOT, 13), (X_DOWN, 12), (D_SLOT, NEAR, 0), (D_SLOT, OWN, 3), (R_SLOT, 1), (Z_RELAY, 14),
+    (D_SLOT, NEAR, 3), (X_UP, 14), (R_SLOT, 4), (D_SLOT, AWAY, 2), (D_SLOT, NEAR, 2), (R_SLOT, 3), (Z_RELAY, 2),
+    (Y_DOWN, OWN, 3), (Y_DOWN, OWN, 0), (D_SLOT, AWAY, 3), (X_DOWN, 14), (Z_RELAY, 1), (X_UP, 4), (Y_DOWN, NEAR, 2),
+    (X_OWN,), (Y_UP, OWN, 2), (D_SLOT, AWAY, 0), (Y_DOWN, NEAR, 0), (D_SLOT, FAR, 3), (R_SLOT, 15), (Y_DOWN, OWN, 1),
+    (Y_UP, NEAR, 0), (X_DOWN, 13), (Y_DOWN, NEAR, 1), (X_DOWN, 0), (Y_UP, OWN, 1), (X_UP, 12), (R_SLOT, 6), (X_UP, 2),
+    (Y_UP, NEAR, 3), (Z_RELAY, 15), (Z_RELAY, 3), (Y_UP, OWN, 0), (Y_UP, NEAR, 2), (Y_DOWN, OWN, 2), (X_UP, 3), (X_UP, 0),
+    (Y_DOWN, AWAY, 3), (D_SLOT, FAR, 2), (Y_DOWN, AWAY, 0), (X_LAST, 14), (R_SLOT, 10), (D_SLOT, AWAY, 1), (R_SLOT, 5),
+    (Z_RELAY, 4), (Y_DOWN, AWAY, 2), (Y_DOWN, FAR, 2), (X_DOWN, 3), (Z_RELAY, 12), (Y_LAST, NEAR, 2), (Y_UP, FAR, 2),
+    (Y_UP, OWN, 3), (X_DOWN, 5), (D_SLOT, FAR, 0), (X_DOWN, 4), (Y_UP, AWAY, 3), (X_UP, 1), (R_SLOT, 11), (X_UP, 15),
+    (X_UP, 10), (Y_UP, NEAR, 1), (R_SLOT, 7), (X_DOWN, 6), (Y_DOWN, FAR, 0), (Y_LAST, OWN, 3), (Y_UP, AWAY, 2),
+    (Y_UP, AWAY, 1), (Y_UP, FAR, 0), (Y_DOWN, NEAR, 3), (Z_RELAY, 13), (R_SLOT, 8), (Y_LAST, OWN, 1), (Y_UP, AWAY, 0),
+    (Y_DOWN, FAR, 3), (X_UP, 11), (X_DOWN, 15), (X_UP, 13), (X_DOWN, 2), (Y_LAST, OWN, 2), (X_DOWN, 11), (X_UP, 5),
+    (X_DOWN, 1), (Y_DOWN, AWAY, 1), (Y_LAST, AWAY, 3), (Y_LAST, OWN, 0), (X_UP, 6), (Y_LAST, NEAR, 0), (R_SLOT, 16),
+    (D_SLOT, FAR, 1), (Y_LAST, NEAR, 3), (Y_UP, FAR, 1), (X_LAST, 3), (X_UP, 8), (Y_LAST, FAR, 2), (Y_UP, FAR, 3),
+    (X_LAST, 15), (Y_LAST, NEAR, 1), (R_SLOT, 9), (X_DOWN, 7), (X_LAST, 13), (X_UP, 7), (X_LAST, 4), (Y_DOWN, FAR, 1),
+    (X_DOWN, 8), (Y_LAST, AWAY, 0), (PREPARE, OWN), (PREPARE, NEAR), (Y_LAST, FAR, 3), (X_LAST, 0), (X_UP, 16),
+    (Y_LAST, AWAY, 2), (X_DOWN, 10), (X_LAST, 2), (X_LAST, 1), (Y_LAST, FAR, 1), (Y_LAST, AWAY, 1), (MULTIPLY, OWN, 3),
+    (X_LAST, 6), (X_DOWN, 16), (X_LAST, 12), (X_UP, 9), (X_DOWN, 9), (Y_LAST, FAR, 0), (MULTIPLY, OWN, 2),
+    (MULTIPLY, NEAR, 2), (X_LAST, 11), (MULTIPLY, NEAR, 3), (MULTIPLY, NEAR, 1), (MULTIPLY, OWN, 0), (MULTIPLY, OWN, 1),
+    (PREPARE, FAR), (X_LAST, 10), (X_LAST, 8), (X_LAST, 5), (PREPARE, AWAY), (X_LAST, 7), (X_LAST, 9), (MULTIPLY, AWAY, 1),
+    (MULTIPLY, AWAY, 2), (MULTIPLY, NEAR, 0), (MULTIPLY, AWAY, 3), (MULTIPLY, FAR, 2), (MULTIPLY, AWAY, 0),
+    (MULTIPLY, FAR, 3), (X_LAST, 16), (MULTIPLY, FAR, 0), (MULTIPLY, FAR, 1),
 ]
 
 PIECES = (
@@ -345,13 +345,20 @@
             PREPARE: prepare,
             MULTIPLY: multiply,
         }
-        for name, *numbers in order:
+        def sent():
+            for copy, when in started:
+                if when is None:
+                    copy.wait_send()
+                else:
+                    pl.when(when)(copy.wait_send)
+
+        quiet = (X_LAST, PREPARE, MULTIPLY)
+        last = max(at for at, step in enumerate(order) if step[0] not in quiet) + 1
+        last = max(last, max(at for at, step in enumerate(order) if step[0] == X_LAST))
+        for at, (name, *numbers) in enumerate(order):
+            if at == last:
+                sent()
             steps[name](*numbers)
-        for copy, when in started:
-            if when is None:
-                copy.wait_send()
-            else:
-                pl.when(when)(copy.wait_send)
 
     edge = jnp.logical_or(p == 0, p == 3)
     pl.when(edge)(lambda: go(EDGE, False))

time: 93.9 us -> 94 us (level)
  no operation moved by 1% of the time
where the time goes in v4:
time: 94 us; the launch traced here: 93.8 us
  Pallas kernels  93 us (99%)
    pallas_call x1, Pallas kernels, body(): pl.pallas_call(kernel, out_shape=jax.ShapeDtypeStruct((512, 256), F32), i...  93 us

profile of v4, /device:TPU:1, one launch (start us, length us, event | category | flops | bytes accessed | tf_op | source)
XLA Modules:
  0.0 93.8 jit_solution(1124776326190723365)
XLA Ops:
  0.0 93.0 %shard_map.28 = f32[512,256]{1,0:T(8,128)S(1)} custom-call(f32[64,1024]{1,0:T(8,128)} %d_hbm.1, f32[64,1024]{1,0:T(8,128)} %r_hbm.1), custom_call_target="tpu_custom_call" | custom-call | tf_op jit(solution)/shard_map/pallas_call | solution.py:371
  93.0 0.8 copy.4
